TPU v7x, 256 devices: a whole 4x4x8 slice. The times are simulated.
256 devices in a mesh: dp: 128 (over z, x_hi, y, core), mp: 2 (over x_lo).
Axes of the slice: x: 4 (x_hi: 2, x_lo: 2; x = x_hi * 2 + x_lo), y: 4, z: 8, core: 2. Of those that a mesh axis runs over, the one named last changes fastest.
Arguments:
- image_feat: bfloat16 [16384, 1024], P('dp', 'mp'), may hold values from -6 to 6
- image_proj: bfloat16 [1024, 768], P('mp'), may hold values from -1 to 1
- text_feat: bfloat16 [16384, 768], P('dp', 'mp'), may hold values from -6 to 6
- text_proj: bfloat16 [768, 768], P('mp'), may hold values from -1 to 1
- pair_index: int32 [16384], P('dp'), may hold values from 0 to 16383, each once
- logit_scale: float32 [1], replicated, may hold values from 10 to 100
Outputs:
- row_loss: float32 [16384], P('dp')
- col_loss: float32 [16384], P(('dp', 'mp'))
Inputs may be any that keep to these rules, and one draw needn't show every extreme that they name: `pair_index`: each text index appears exactly once.
All inputs are finite; a program needn't handle non-finite values.
Results may differ from a plain program's by a relative error of at most 0.00091.
Values may be sent and summed in bfloat16 or wider, within the bound.
A program may use at most 64 MiB of HBM per device.

v0:
```python
import jax
import jax.numpy as jnp
from jax import lax
from jax.sharding import PartitionSpec as P


def copy_for_each(value, axis):
    copies = jnp.broadcast_to(value, (lax.axis_size(axis), *value.shape))
    return lax.all_to_all(copies, axis, split_axis=0, concat_axis=0, tiled=True)


def taken_together(value, axis):
    everything = copy_for_each(value, axis)
    return jnp.sum(everything, axis=0)


def cut_along(value, dim, length):
    dims = value.shape
    tiles = value.reshape(*dims[:dim], length, dims[dim] // length, *dims[dim + 1 :])
    return jnp.moveaxis(tiles, dim, 0)


def summed_on_arrival(value, axis, dim):
    length = lax.axis_size(axis)
    tiles = lax.all_to_all(cut_along(value, dim, length), axis, 0, 0, tiled=True)
    return jnp.sum(tiles, axis=0)


def all_in_one(value, axis):
    leaves = jax.tree.leaves(value)
    sequence = sorted(range(len(leaves)), key=lambda k: -leaves[k].size)
    width = (1, *leaves[sequence[0]].shape)[-1]
    lines = [
        jnp.pad(leaves[k].reshape(-1), (0, -leaves[k].size % width)).reshape(-1, width)
        for k in sequence
    ]
    both, at, found = (lax.all_gather(jnp.concatenate(lines), axis), 0, {})
    for k, line in zip(sequence, lines):
        slab = both[:, at : at + len(line)].reshape(len(both), -1)
        found[k] = slab[:, : leaves[k].size].reshape(-1, *leaves[k].shape)
        at += len(line)
    numbers = iter(range(len(leaves)))
    return jax.tree.map(lambda _: found[next(numbers)], value)


def joined(part, axis, combine):
    gathered = all_in_one(part, axis)

    def take(source):
        return jax.tree.map(lambda a: lax.dynamic_index_in_dim(a, source, 0, False), gathered)

    return lax.fori_loop(
        1, lax.axis_size(axis), lambda source, state: combine(state, take(source)), take(0)
    )


def side_by_side(arrays, axis, split_dim, concat_dim, along):
    both = jnp.concatenate(arrays, axis=along)
    out, at, outs = (
        lax.all_to_all(both, axis, split_axis=split_dim, concat_axis=concat_dim, tiled=True),
        0,
        [],
    )
    for a in arrays:
        outs.append(lax.slice_in_dim(out, at, at + a.shape[along], axis=along))
        at += a.shape[along]
    return tuple(outs)


def normalize(raw):
    norm_sq = jnp.sum(raw * raw, axis=1, keepdims=True)
    return (raw / jnp.sqrt(norm_sq + 1e-06)).astype(jnp.bfloat16)


def combine_stats(first, second):
    top = jnp.maximum(first[0], second[0])
    total = first[1] * jnp.exp(first[0] - top) + second[1] * jnp.exp(second[0] - top)
    return (top, total, first[2] + second[2])


def on_device(image_feat, image_proj, text_feat, text_proj, pair_index, logit_scale):
    multiplier = logit_scale[0]
    image_part = jnp.dot(image_feat, image_proj, preferred_element_type=jnp.float32)
    image_emb = normalize(taken_together(image_part, "mp"))
    text_part = jnp.dot(text_feat, text_proj, preferred_element_type=jnp.float32)
    mp_count = lax.axis_size("mp")
    mp_index = lax.axis_index("mp")
    row_count = text_part.shape[0]
    half_rows = row_count // mp_count
    own_text = summed_on_arrival(text_part, "mp", 0)
    text_emb = normalize(own_text)
    dp_count = lax.axis_size("dp")
    piece = lax.all_gather(text_emb, "dp", axis=0, tiled=True)
    row_max = jnp.full((row_count,), -jnp.inf, jnp.float32)
    row_sum = jnp.zeros((row_count,), jnp.float32)
    width_now = piece.shape[0]
    logits = multiplier * lax.dot_general(
        image_emb, piece, (((1,), (1,)), ((), ())), preferred_element_type=jnp.float32
    )
    local_idx = jnp.arange(width_now, dtype=jnp.int32)
    global_idx = local_idx // half_rows * row_count + mp_index * half_rows + local_idx % half_rows
    matched = pair_index[:, None] == global_idx[None, :]
    picked = jnp.where(matched, logits, 0.0)
    new_max = jnp.max(logits, axis=1)
    row_sum = row_sum * jnp.exp(row_max - new_max) + jnp.sum(
        jnp.exp(logits - new_max[:, None]), axis=1
    )
    row_pos = jnp.sum(picked, axis=1)
    block_max = jnp.max(logits, axis=0)
    block_sum = jnp.sum(jnp.exp(logits - block_max[None, :]), axis=0)
    block_pos = jnp.sum(picked, axis=0)
    col_max = block_max
    col_sum = block_sum
    col_pos = block_pos
    row_max, row_sum, row_pos, col_max, col_sum, col_pos = (
        new_max,
        row_sum,
        row_pos,
        col_max,
        col_sum,
        col_pos,
    )
    row_max, row_sum, row_pos = joined((row_max, row_sum, row_pos), "mp", combine_stats)
    row_loss = row_max + jnp.log(row_sum) - row_pos
    shaped_max = col_max.reshape(dp_count, half_rows)
    shaped_sum = col_sum.reshape(dp_count, half_rows)
    shaped_pos = col_pos.reshape(dp_count, half_rows)
    got_max, got_sum, got_pos = side_by_side((shaped_max, shaped_sum, shaped_pos), "dp", 0, 0, 1)
    top = jnp.max(got_max, axis=0)
    total = jnp.sum(got_sum * jnp.exp(got_max - top[None, :]), axis=0)
    positive = jnp.sum(got_pos, axis=0)
    col_loss = top + jnp.log(total) - positive
    return (row_loss, col_loss)


def solution(mesh):
    in_specs = (P("dp", "mp"), P("mp", None), P("dp", "mp"), P("mp", None), P("dp"), P())
    out_specs = (P("dp"), P(("dp", "mp")))
    return jax.shard_map(
        on_device, mesh=mesh, in_specs=in_specs, out_specs=out_specs, check_vma=False
    )
```

profile of v0, /device:TPU:1, one launch (start us, length us, event | category | flops | bytes accessed | tf_op | source)
XLA Modules:
  0.0 208.7 jit_solution(853077514270818465)
XLA Ops:
  7.2 0.0 copy-start
  7.2 0.0 all-gather.4.cloned.1.call-start
  7.2 1.4 fusion.23
  8.7 7.8 %all_to_all.22 = f32[2,64,768]{2,1,0:T(8,128)S(1)} all-to-all(f32[2,64,768]{2,1,0:T(8,128)S(1)} %bitcast.46), channel_id=1, replica_groups=mesh['dp'=128,'mp'=2] {'mp'}, dimensions={0} | all-to-all | bytes 786432 | tf_op jit(solution)/shard_map/all_to_all | solution.py:25
  16.5 0.1 multiply_reduce_fusion.1
  16.6 0.7 divide_convert_fusion.2
  17.4 0.0 all-gather.4.cloned.1.call-update
  17.4 0.0 copy-done
  17.4 1.2 fusion.22
  18.6 1.0 broadcast_in_dim.10
  19.6 3.5 %all-to-all-start = ((f32[2,128,768]{2,1,0:T(8,128)}), f32[2,128,768]{2,1,0:T(8,128)S(1)}, u32[]{:S(2)}, u32[]{:S(2)}) async-start(f32[2,128,768]{2,1,0:T(8,128)} %broadcast_in_dim.10), calls=%async_computation | async-start | bytes 1572864 | tf_op jit(solution)/shard_map/all_to_all | solution.py:9
  23.8 6.5 %all-to-all-done = f32[2,128,768]{2,1,0:T(8,128)S(1)} async-done(((f32[2,128,768]{2,1,0:T(8,128)}), f32[2,128,768]{2,1,0:T(8,128)S(1)}, u32[]{:S(2)}, u32[]{:S(2)}) %all-to-all-start) | async-done | bytes 786464 | tf_op jit(solution)/shard_map/all_to_all | solution.py:9
  30.3 0.1 reduce_sum.92
  30.4 0.1 multiply_reduce_fusion
  30.5 131.8 %all-gather.4.cloned.1.call-done = bf16[8192,768]{1,0:T(8,128)(2,1)} async-done(((bf16[64,768]{1,0:T(8,128)(2,1)}), bf16[8192,768]{1,0:T(8,128)(2,1)}) %all-gather.4.cloned.1.call-update) | async-done | bytes 12582928 | tf_op jit(solution)/shard_map/all_gather | solution.py:93
  162.3 8.8 %fusion.21 = (f32[128]{0:T(128)S(1)}, f32[128,8192]{1,0:T(8,128)S(1)}) fusion(bf16[8192,768]{1,0:T(8,128)(2,1)} %all-gather.4.cloned.1.call-done, f32[128,768]{1,0:T(8,128)S(1)} %reduce_sum.92, f32[128]{0:T(128)S(1)} %add_sqrt_fusion.1, f32[]{:T(128)} %bitcast.45), kind=kOutput, calls=%fused_computation.48 | convolution fusion | flops 1612906368 | bytes 17171460 | tf_op jit(solution)/shard_map/dot_general | solution.py:97
  171.2 0.0 copy-start.1
  171.2 0.0 copy-start.2
  171.2 1.9 copy-done.1
  173.1 1.1 fusion.20
  174.2 0.1 reshape.103
  174.2 0.0 copy-done.2
  174.2 3.6 %fusion = (f32[8192]{0:T(1024)S(1)}, f32[128]{0:T(128)S(1)}, f32[8192]{0:T(1024)S(1)}) fusion(f32[128,8192]{1,0:T(8,128)} %copy-done.1, s32[8192]{0:T(1024)S(1)} %fusion.11, s32[128]{0:T(128)S(1)} %copy-done.2, f32[8192]{0:T(1024)S(1)} %get-tuple-element.21), kind=kLoop, calls=%fused_computation.4 | loop fusion | flops 6274944 | bytes 4326400 | tf_op jit(solution)/shard_map/reduce_sum | solution.py:111
  177.9 0.1 reshape.104
  177.9 0.1 reshape.105
  178.0 0.1 maximum_bitcast_fusion
  178.1 0.8 copy.11
  178.9 8.4 %all-to-all-start.2 = ((f32[128,1,192]{2,1,0:T(1,128)}), f32[128,1,192]{2,1,0:T(1,128)S(1)}, u32[]{:S(2)}, u32[]{:S(2)}) async-start(f32[128,1,192]{2,1,0:T(1,128)} %copy.11), calls=%async_computation.2 | async-start | bytes 262144 | tf_op jit(solution)/shard_map/all_to_all | solution.py:60
  187.4 3.2 %all-gather.1 = f32[2,3,128]{2,1,0:T(4,128)S(1)} all-gather(f32[1,3,128]{2,1,0:T(4,128)S(1)} %maximum_bitcast_fusion.1), channel_id=2, replica_groups=mesh['dp'=128,'mp'=2] {'mp'}, dimensions={0}, use_global_device_ids=true | all-gather | bytes 4608 | tf_op jit(solution)/shard_map/all_gather | solution.py:37
  190.6 0.5 fusion.15
  191.1 9.8 %all-to-all-done.2 = f32[128,1,192]{2,1,0:T(1,128)S(1)} async-done(((f32[128,1,192]{2,1,0:T(1,128)}), f32[128,1,192]{2,1,0:T(1,128)S(1)}, u32[]{:S(2)}, u32[]{:S(2)}) %all-to-all-start.2) | async-done | bytes 98336 | tf_op jit(solution)/shard_map/all_to_all | solution.py:60
  200.9 0.1 copy.12
  201.0 0.1 slice_reduce_fusion.1
  201.1 0.2 fusion.13
  201.3 0.5 add_subtract_fusion
  (6 shorter events, 0.1 us)
Async XLA Ops:
  7.2 10.2 %copy-start = (bf16[512,768]{1,0:T(8,128)(2,1)S(1)}, bf16[512,768]{1,0:T(8,128)(2,1)}, u32[]{:S(2)}) copy-start(bf16[512,768]{1,0:T(8,128)(2,1)} %param.7) | copy-start | bytes 2359300
  7.2 155.1 %all-gather.4.cloned.1.call-start = ((), (), s32[]{:S(2)}) async-start(), calls=%async_computation.3 | async-start | bytes 12681216 | tf_op jit(solution)/shard_map/all_gather | solution.py:93
  19.6 10.8 %all-to-all-start = ((f32[2,128,768]{2,1,0:T(8,128)}), f32[2,128,768]{2,1,0:T(8,128)S(1)}, u32[]{:S(2)}, u32[]{:S(2)}) async-start(f32[2,128,768]{2,1,0:T(8,128)} %broadcast_in_dim.10), calls=%async_computation | async-start | bytes 1572864 | tf_op jit(solution)/shard_map/all_to_all | solution.py:9
  171.2 1.9 copy-start.1
  171.2 3.1 %copy-start.2 = (s32[128]{0:T(128)S(1)}, s32[128]{0:T(128)}, u32[]{:S(2)}) copy-start(s32[128]{0:T(128)} %param.10) | copy-start | bytes 1540
  178.9 22.0 %all-to-all-start.2 = ((f32[128,1,192]{2,1,0:T(1,128)}), f32[128,1,192]{2,1,0:T(1,128)S(1)}, u32[]{:S(2)}, u32[]{:S(2)}) async-start(f32[128,1,192]{2,1,0:T(1,128)} %copy.11), calls=%async_computation.2 | async-start | bytes 262144 | tf_op jit(solution)/shard_map/all_to_all | solution.py:60
Sparse Core Ops, SparseCore 0:
  17.5 144.7 all-gather.3
where the time goes:
time: 209 us
  waiting for transfers between devices  148 us (71%)
  between operations  14.8 us (7%)
  starting transfers between devices  12 us (6%)
  matrix products  11.5 us (6%)
  blocking collectives  11 us (5%)
  other arithmetic  7.22 us (3%)
  local copies, waits for them, and re-layouts  3.99 us (2%)
    all_gather x1, waiting for transfers between devices, on_device(): piece = lax.all_gather(text_emb, 'dp', axis=0, tiled=True)  132 us
    all_to_all x1, waiting for transfers between devices, side_by_side(): lax.all_to_all(both, axis, split_axis=split_dim, concat_axis=concat_dim,...  9.77 us
    dot_general x1, matrix products, on_device(): lax.dot_general(image_emb, piece, (((1,), (1,)), ((), ())), preferred_ele...  8.84 us
    all_to_all x1, starting transfers between devices, side_by_side(): lax.all_to_all(both, axis, split_axis=split_dim, concat_axis=concat_dim,...  8.42 us
    all_to_all x1, blocking collectives, summed_on_arrival(): lax.all_to_all(cut_along(value, dim, length), axis, 0, 0, tiled=True)  7.82 us
    all_to_all x1, waiting for transfers between devices, copy_for_each(): return lax.all_to_all(copies, axis, split_axis=0, concat_axis=0, tiled=True)  6.54 us
  transfers between devices with their start and end apart: 3, of which 3 were waited for; matrix products, arithmetic and copies ran while one was open for 1% of the time, Pallas kernels for 0%

commit v1 on v0

v1 whole, which is shorter than its diff:
```python
import functools
import math

import jax
import jax.numpy as jnp
from jax import lax
from jax.experimental import pallas as pl
from jax.experimental.pallas import tpu as pltpu
from jax.sharding import PartitionSpec as P

MESH = pl.DeviceIdType.MESH
F32 = jnp.float32
BF16 = jnp.bfloat16

NX, NY, NZ, NC = 4, 4, 8, 2
ROWS = 64
EMB = 768
TILE = 1024
HIGH, LOW, CLAMP = 34.0, 20.0, 90.0
LN2 = math.log(2.0)


def device(x, y, z, c):
    dp = ((z * 2 + lax.div(x, 2)) * NY + y) * NC + c
    return (dp, lax.rem(x, 2))


def kernel(
    fi_hbm, pi_hbm, ft_hbm, pt_hbm, pair_hbm, scale_ref,
    row_ref, col_ref,
    fi, pi, ft, pt, part_i, part_t, send_i, send_t, got_i, got_t,
    img, txt, pair, logit, colsum, rowstat, colstat, rows_in, cols_in,
    load_sem, exch_send, exch_recv, img_send, img_recv, txt_send, txt_recv,
    pair_send, pair_recv, rs_send, rs_recv, cs_send, cs_recv,
):
    dp, mp = lax.axis_index("dp"), lax.axis_index("mp")
    c = lax.rem(dp, 2)
    y = lax.rem(lax.div(dp, 2), NY)
    xh = lax.rem(lax.div(dp, 8), 2)
    z = lax.div(dp, 16)
    x = xh * 2 + mp
    shard = xh * NY + y
    slot = shard * 2 + mp
    cslot = c * NZ + z

    def slot_of(xx, yy):
        return (lax.div(xx, 2) * NY + yy) * 2 + lax.rem(xx, 2)

    loads = []
    for k, (src, dst) in enumerate(((fi_hbm, fi), (pi_hbm, pi), (ft_hbm, ft), (pt_hbm, pt), (pair_hbm, pair.at[shard]))):
        copy = pltpu.make_async_copy(src, dst, load_sem.at[k])
        copy.start()
        loads.append(copy)

    plane = []
    for dx in range(NX):
        for dy in range(NY):
            if dx or dy:
                plane.append((lax.rem(x + dx, NX), lax.rem(y + dy, NY)))
    column = []
    for dz in range(NZ):
        for dc in range(NC):
            if dz or dc:
                column.append((lax.rem(z + dz, NZ), lax.rem(c + dc, NC)))

    barrier = pltpu.get_barrier_semaphore()
    for px, py in plane:
        pl.semaphore_signal(barrier, inc=1, device_id=device(px, py, z, c), device_id_type=MESH)
    for pz, pc in column:
        pl.semaphore_signal(barrier, inc=1, device_id=device(x, y, pz, pc), device_id_type=MESH)

    started = []

    def send(src, dst, send_sem, recv_sem, to):
        copy = pltpu.make_async_remote_copy(
            src_ref=src, dst_ref=dst, send_sem=send_sem, recv_sem=recv_sem, device_id=to, device_id_type=MESH
        )
        copy.start()
        started.append(copy)

    sibling = device(x, y, z, 1 - c)

    def arrived(dst, recv_sem):
        pltpu.make_async_remote_copy(
            src_ref=dst, dst_ref=dst, send_sem=exch_send.at[0], recv_sem=recv_sem, device_id=sibling, device_id_type=MESH
        ).wait_recv()

    own = pl.ds(pl.multiple_of(mp * ROWS, ROWS), ROWS)
    other = pl.ds(pl.multiple_of((1 - mp) * ROWS, ROWS), ROWS)
    partner = device(xh * 2 + 1 - mp, y, z, c)

    loads[0].wait()
    loads[1].wait()
    part_i[...] = jnp.dot(fi[...], pi[...], preferred_element_type=F32)
    send_i[...] = part_i[other, :].astype(BF16)
    pl.semaphore_wait(barrier, len(plane) + len(column))
    send(send_i, got_i, exch_send.at[0], exch_recv.at[0], partner)
    loads[2].wait()
    loads[3].wait()
    part_t[...] = jnp.dot(ft[...], pt[...], preferred_element_type=F32)
    send_t[...] = part_t[other, :].astype(BF16)
    send(send_t, got_t, exch_send.at[1], exch_recv.at[1], partner)
    loads[4].wait()
    n_pair = 0
    for px, py in plane:
        pass
    for dxh in range(2):
        for dy in range(NY):
            if dxh or dy:
                to = device(lax.rem(xh + dxh, 2) * 2 + mp, lax.rem(y + dy, NY), z, c)
                send(pair.at[shard], pair.at[shard], pair_send.at[n_pair], pair_recv.at[shard], to)
                n_pair += 1

    def normalize(raw):
        norm_sq = jnp.sum(raw * raw, axis=1, keepdims=True)
        return (raw / jnp.sqrt(norm_sq + 1e-06)).astype(BF16)

    def img_at(s, half):
        return img.at[pl.ds(pl.multiple_of(s * ROWS + half * 32, 32), 32), :]

    def txt_at(cs, zs, half):
        return txt.at[pl.ds(pl.multiple_of((cs * NZ + zs) * ROWS + half * 32, 32), 32), :]

    count = {"img": 0, "txt": 0}

    def send_img(s, half, to):
        send(img_at(s, half), img_at(s, half), img_send.at[count["img"]], img_recv.at[s * 2 + half], to)
        count["img"] += 1

    def send_txt(cs, zs, half, to):
        send(
            txt_at(cs, zs, half), txt_at(cs, zs, half), txt_send.at[count["txt"]],
            txt_recv.at[(cs * NZ + zs) * 2 + half], to,
        )
        count["txt"] += 1

    along_x = [device(lax.rem(x + d, NX), y, z, c) for d in (1, 3, 2)]
    along_y = [device(x, lax.rem(y + d, NY), z, c) for d in (1, 3, 2)]
    up, down = device(x, y, lax.rem(z + 1, NZ), c), device(x, y, lax.rem(z + NZ - 1, NZ), c)

    arrived(got_i, exch_recv.at[0])
    img[pl.ds(pl.multiple_of(slot * ROWS, ROWS), ROWS), :] = normalize(part_i[own, :] + got_i[...].astype(F32))
    for kx, ky in zip(along_x, along_y):
        send_img(slot, 0, kx)
        send_img(slot, 1, ky)
    for kx, ky in zip(along_x, along_y):
        send_img(slot, 0, ky)
        send_img(slot, 1, kx)

    arrived(got_t, exch_recv.at[1])
    txt[pl.ds(pl.multiple_of(cslot * ROWS, ROWS), ROWS), :] = normalize(part_t[own, :] + got_t[...].astype(F32))
    for half in range(2):
        send_txt(c, z, half, up)
        send_txt(c, z, half, down)
    for half in range(2):
        send_txt(c, z, half, sibling)

    def relay_img(d):
        sx = slot_of(lax.rem(x + d, NX), y)
        arrived(img_at(sx, 0), img_recv.at[sx * 2])
        for ky in along_y:
            send_img(sx, 0, ky)
        sy = slot_of(x, lax.rem(y + d, NY))
        arrived(img_at(sy, 1), img_recv.at[sy * 2 + 1])
        for kx in along_x:
            send_img(sy, 1, kx)

    def relay_txt(k, half):
        below, above = lax.rem(z + NZ - k, NZ), lax.rem(z + k, NZ)
        if k < 4 or half == 0:
            arrived(txt_at(c, below, half), txt_recv.at[(c * NZ + below) * 2 + half])
            if k < 3 or (k == 3 and half == 0):
                send_txt(c, below, half, up)
            send_txt(c, below, half, sibling)
        if k < 4 or half == 1:
            arrived(txt_at(c, above, half), txt_recv.at[(c * NZ + above) * 2 + half])
            if k < 3 or (k == 3 and half == 1):
                send_txt(c, above, half, down)
            send_txt(c, above, half, sibling)

    relay_img(1)
    relay_img(3)
    relay_txt(1, 0)
    relay_txt(1, 1)
    relay_img(2)
    for k in (2, 3, 4):
        relay_txt(k, 0)
        relay_txt(k, 1)

    for dx in range(1, NX):
        for dy in range(1, NY):
            s = slot_of(lax.rem(x + dx, NX), lax.rem(y + dy, NY))
            for half in range(2):
                arrived(img_at(s, half), img_recv.at[s * 2 + half])
    for d in range(1, NX):
        sx = slot_of(lax.rem(x + d, NX), y)
        arrived(img_at(sx, 1), img_recv.at[sx * 2 + 1])
        sy = slot_of(x, lax.rem(y + d, NY))
        arrived(img_at(sy, 0), img_recv.at[sy * 2])
    for zs in range(NZ):
        for half in range(2):
            arrived(txt_at(1 - c, zs, half), txt_recv.at[((1 - c) * NZ + zs) * 2 + half])
    for dxh in range(2):
        for dy in range(NY):
            if dxh or dy:
                q = lax.rem(xh + dxh, 2) * NY + lax.rem(y + dy, NY)
                arrived(pair.at[q], pair_recv.at[q])

    scale = scale_ref[0]
    to_log2 = scale * (1.0 / LN2)
    sub = lax.broadcasted_iota(jnp.int32, (32, 128), 0)
    zero = jnp.zeros((8, 128), F32)
    row_a, row_b, row_p = [zero] * 8, [zero] * 8, [zero] * 8
    step = 256
    for m in range(TILE // step):
        buf = m % 2
        logit[buf] = lax.dot_general(
            txt[m * step : (m + 1) * step, :], img[...], (((1,), (1,)), ((), ())), preferred_element_type=F32
        )
        for g in range(step // 32):
            at = m * step + g * 32
            cs, zs, r = at // 512, at // 64 % 8, at % 64
            text = sub + (zs * 2048 + cs * 128 + r) + (xh * 1024 + y * 256 + mp * 64)
            col_a = col_b = col_p = jnp.zeros((32, 128), F32)
            for q in range(8):
                acc = logit[buf, g * 32 : (g + 1) * 32, q * 128 : (q + 1) * 128]
                power = acc * to_log2
                a = jnp.exp2(power - HIGH)
                b = jnp.exp2(jnp.minimum(power, CLAMP) + LOW)
                p = jnp.where(pair[q] == text, acc, 0.0)
                col_a, col_b, col_p = col_a + a, col_b + b, col_p + p
                row_a[q] = row_a[q] + a.reshape(4, 8, 128).sum(axis=0)
                row_b[q] = row_b[q] + b.reshape(4, 8, 128).sum(axis=0)
                row_p[q] = row_p[q] + p.reshape(4, 8, 128).sum(axis=0)
            colsum[0, at : at + 32, :] = col_a
            colsum[1, at : at + 32, :] = col_b
            colsum[2, at : at + 32, :] = col_p

    line = lax.broadcasted_iota(jnp.int32, (8, 128), 0)

    def three(a, b, p):
        return jnp.where(line == 0, a, jnp.where(line == 1, b, jnp.where(line == 2, p, 0.0)))

    for q in range(8):
        sums = [jnp.sum(v[q], axis=0, keepdims=True) for v in (row_a, row_b, row_p)]
        rowstat[q] = three(*sums)
    for n, (px, py) in enumerate(plane):
        q = lax.div(px, 2) * NY + py
        send(rowstat.at[q], rows_in.at[slot], rs_send.at[n], rs_recv.at[slot], device(px, py, z, c))
    for blk in range(8):
        sums = [
            jnp.sum(colsum[k, blk * 128 : (blk + 1) * 128, :].T, axis=0, keepdims=True) for k in range(3)
        ]
        colstat[blk] = three(*sums)
    for n, (pz, pc) in enumerate(column):
        blk = pc * 4 + lax.div(pz, 2)
        send(colstat.at[blk], cols_in.at[cslot], cs_send.at[n], cs_recv.at[cslot], device(x, y, pz, pc))

    def loss(total):
        high, low, positive = total[0:1], total[1:2], total[2:3]
        lse = jnp.where(high > 2.0**-HIGH, jnp.log(high) + HIGH * LN2, jnp.log(low) - LOW * LN2)
        return lse - scale * positive

    total = rowstat[shard]
    for px, py in plane:
        s = slot_of(px, py)
        arrived(rows_in.at[s], rs_recv.at[s])
        total = total + rows_in[s]
    row_ref[...] = loss(total)
    total = colstat[c * 4 + lax.div(z, 2)]
    for pz, pc in column:
        s = pc * NZ + pz
        arrived(cols_in.at[s], cs_recv.at[s])
        total = total + cols_in[s]
    both = loss(total)
    col_ref[...] = jnp.where(lax.rem(z, 2) == 0, both[:, :ROWS], both[:, ROWS:])

    for copy in started:
        copy.wait_send()


def on_device(image_feat, image_proj, text_feat, text_proj, pair_index, logit_scale):
    dma = pltpu.SemaphoreType.DMA
    anywhere = pl.BlockSpec(memory_space=pl.ANY)
    vmem = pl.BlockSpec(memory_space=pltpu.VMEM)
    row, col = pl.pallas_call(
        kernel,
        out_shape=(jax.ShapeDtypeStruct((1, 2 * ROWS), F32), jax.ShapeDtypeStruct((1, ROWS), F32)),
        in_specs=[anywhere] * 5 + [pl.BlockSpec(memory_space=pltpu.SMEM)],
        out_specs=(vmem, vmem),
        scratch_shapes=[
            pltpu.VMEM(image_feat.shape, BF16),
            pltpu.VMEM(image_proj.shape, BF16),
            pltpu.VMEM(text_feat.shape, BF16),
            pltpu.VMEM(text_proj.shape, BF16),
            pltpu.VMEM((2 * ROWS, EMB), F32),
            pltpu.VMEM((2 * ROWS, EMB), F32),
            pltpu.VMEM((ROWS, EMB), BF16),
            pltpu.VMEM((ROWS, EMB), BF16),
            pltpu.VMEM((ROWS, EMB), BF16),
            pltpu.VMEM((ROWS, EMB), BF16),
            pltpu.VMEM((TILE, EMB), BF16),
            pltpu.VMEM((TILE, EMB), BF16),
            pltpu.VMEM((8, 1, 128), jnp.int32),
            pltpu.VMEM((2, 256, TILE), F32),
            pltpu.VMEM((3, TILE, 128), F32),
            pltpu.VMEM((8, 8, 128), F32),
            pltpu.VMEM((8, 8, 128), F32),
            pltpu.VMEM((16, 8, 128), F32),
            pltpu.VMEM((16, 8, 128), F32),
            dma((5,)), dma((2,)), dma((2,)), dma((30,)), dma((32,)), dma((30,)), dma((32,)),
            dma((7,)), dma((8,)), dma((15,)), dma((16,)), dma((15,)), dma((16,)),
        ],
        compiler_params=pltpu.CompilerParams(
            collective_id=0, has_side_effects=True, vmem_limit_bytes=60 * 1024 * 1024
        ),
        name="contrastive",
    )(image_feat, image_proj, text_feat, text_proj, pair_index.reshape(1, 2 * ROWS), logit_scale)
    return row.reshape(2 * ROWS), col.reshape(ROWS)


def solution(mesh):
    in_specs = (P("dp", "mp"), P("mp", None), P("dp", "mp"), P("mp", None), P("dp"), P())
    out_specs = (P("dp"), P(("dp", "mp")))
    return jax.shard_map(on_device, mesh=mesh, in_specs=in_specs, out_specs=out_specs, check_vma=False)
```

time: 209 us -> 46.7 us (0.22)
  waiting for transfers between devices: 148 us -> 0 us
  Pallas kernels: 0 us -> 43.5 us
  between operations: 14.8 us -> 1.3 us
  starting transfers between devices: 12 us -> 0 us
  matrix products: 11.5 us -> 0 us
  blocking collectives: 11 us -> 0 us
  other arithmetic: 7.22 us -> 0 us
  local copies, waits for them, and re-layouts: 3.99 us -> 1.8 us
    all_gather x1 -> x0, waiting for transfers between devices: 132 us -> none  [on_device(): piece = lax.all_gather(text_emb, 'dp', axis=0, tiled=True)]
    pallas_call x0 -> x1, Pallas kernels: none -> 43.5 us  [on_device(): pl.pallas_call(kernel, out_shape=(jax.ShapeDtypeStruct((1, 2 * ROWS), F32...]
    all_to_all x2 -> x0, waiting for transfers between devices: 16.3 us -> none  [the longest x1 9.77 us: side_by_side(): lax.all_to_all(both, axis, split_axis=split_dim, concat_axis=concat_dim,...]
    all_to_all x2 -> x0, starting transfers between devices: 12 us -> none  [the longest x1 8.42 us: side_by_side(): lax.all_to_all(both, axis, split_axis=split_dim, concat_axis=concat_dim,...]
    dot_general x3 -> x0, matrix products: 11.5 us -> none  [the longest x1 8.84 us: on_device(): lax.dot_general(image_emb, piece, (((1,), (1,)), ((), ())), preferred_ele...]
    all_to_all x1 -> x0, blocking collectives: 7.82 us -> none  [summed_on_arrival(): lax.all_to_all(cut_along(value, dim, length), axis, 0, 0, tiled=True)]
    reduce_sum x6 -> x0, other arithmetic: 4.11 us -> none  [the longest x1 3.62 us: on_device(): block_pos = jnp.sum(picked, axis=0)]
    all_gather x1 -> x0, blocking collectives: 3.21 us -> none  [all_in_one(): both, at, found = (lax.all_gather(jnp.concatenate(lines), axis), 0, {})]
  transfers between devices with their start and end apart: 3 -> 0, of which waited for: 3 -> 0; matrix products, arithmetic and copies ran while one was open for 1% -> 0% of each run, Pallas kernels for 0% -> 0%
where the time goes in v1:
time: 46.7 us; the launch traced here: 46.6 us
  Pallas kernels  43.5 us (93%)
  local copies, waits for them, and re-layouts  1.8 us (4%)
  between operations  1.3 us (3%)
    pallas_call x1, Pallas kernels, on_device(): pl.pallas_call(kernel, out_shape=(jax.ShapeDtypeStruct((1, 2 * ROWS), F32...  43.5 us
    unnamed x6, local copies, waits for them, and re-layouts  1.8 us

profile of v1, /device:TPU:1, one launch (start us, length us, event | category | flops | bytes accessed | tf_op | source)
XLA Modules:
  0.0 46.6 jit_solution(6681987476666477472)
XLA Ops:
  1.3 43.5 %contrastive.1 = (f32[1,128]{1,0:T(1,128)}, f32[1,64]{1,0:T(1,128)}) custom-call(bf16[128,512]{1,0:T(8,128)(2,1)} %fi_hbm.1, bf16[512,768]{1,0:T(8,128)(2,1)} %pi_hbm.1, bf16[128,384]{1,0:T(8,128)(2,1)} %ft_hbm.1, bf16[384,768]{1,0:T(8,128)(2,1)} %pt_hbm.1, s32[1,128]{1,0:T(1,128)} %bitcast.3, f32[1]{0:T(128)S(6)} %copy.10.scale_ref), custom_call_target="tpu_custom_call" | custom-call | tf_op jit(solution)/shard_map/contrastive/pallas_call | solution.py:286
  44.8 0.0 copy-start.1
  44.8 0.7 %copy-done.1 = f32[1,128]{1,0:T(1,128)S(1)} copy-done((f32[1,128]{1,0:T(1,128)S(1)}, f32[1,128]{1,0:T(1,128)}, u32[]{:S(2)}) %copy-start.1) | copy-done | bytes 536
  45.4 0.0 copy-start
  45.4 0.5 %copy.11 = f32[128]{0:T(128)} copy(f32[128]{0:T(128)S(1)} %bitcast.5) | data formatting | bytes 1024
  46.0 0.1 copy-done
  46.1 0.5 %copy.12 = f32[64]{0:T(128)} copy(f32[64]{0:T(128)S(1)} %bitcast.4) | data formatting | bytes 512
Async XLA Ops:
  44.8 0.7 %copy-start.1 = (f32[1,128]{1,0:T(1,128)S(1)}, f32[1,128]{1,0:T(1,128)}, u32[]{:S(2)}) copy-start(f32[1,128]{1,0:T(1,128)} %get-tuple-element.4) | copy-start | bytes 1540
  45.4 0.6 %copy-start = (f32[1,64]{1,0:T(1,128)S(1)}, f32[1,64]{1,0:T(1,128)}, u32[]{:S(2)}) copy-start(f32[1,64]{1,0:T(1,128)} %get-tuple-element.5) | copy-start | bytes 772
